TPU v7x, 32 devices: a whole 2x2x4 slice. The times are simulated.
32 devices in a mesh: grp: 4 (over y, x), chan: 8 (over z, core).
Axes of the slice: x: 2, y: 2, z: 4, core: 2. Of those that a mesh axis runs over, the one named last changes fastest.
Arguments:
- visibility: float32 [1024, 32768], P('chan', 'grp'), may hold values from -6 to 6
- interference_mask: int32 [1024, 16384], P(None, ('grp', 'chan')), may hold values from 0 to 1
- valid_time_count: int32 [512], P(('grp', 'chan')), may hold values from 8 to 32
- fit_modes: float32 [1024, 32], P('grp'), may hold values from -1 to 1
Outputs:
- residual_vis: float32 [1024, 32768], P('chan', 'grp')
All inputs are finite; a program needn't handle non-finite values.
Results may differ from a plain program's by a relative error of at most 0.0003.
Values sent between devices are 32-bit elements; how exact they have to be, the bound alone decides.
A program may use at most 128 MiB of HBM per device.

v0:
```python
import functools

import jax
import jax.numpy as jnp
from jax import lax
from jax.experimental import pallas as pl
from jax.experimental.pallas import tpu as pltpu
from jax.sharding import PartitionSpec as P

damping = 0.1
LANES = 128
VMEM = pl.BlockSpec(memory_space=pltpu.VMEM)
MESH = pl.DeviceIdType.MESH


def factor_kernel(mt_ref, mask_ref, valid_ref, spread_ref, l_ref, inv_ref, w_ref, hi_ref, mid_ref, lo_ref):
    modes, freqs = mt_ref.shape
    columns = mask_ref.shape[1]
    for j in range(columns // LANES):
        part = slice(j * LANES, (j + 1) * LANES)
        w = (1.0 - mask_ref[:, part].astype(jnp.float32)) * valid_ref[:, part]
        w_ref[:, 2 * j * LANES : 2 * (j + 1) * LANES] = jnp.dot(
            w.astype(jnp.bfloat16), spread_ref[...], preferred_element_type=jnp.float32
        ).astype(jnp.bfloat16)

    def split(i, carry):
        pair = mt_ref[...] * mt_ref[pl.ds(i, 1), :]
        rows = pl.ds(pl.multiple_of(i * modes, modes), modes)
        hi = pair.astype(jnp.bfloat16)
        rest = pair - hi.astype(jnp.float32)
        mid = rest.astype(jnp.bfloat16)
        hi_ref[rows, :] = hi
        mid_ref[rows, :] = mid
        lo_ref[rows, :] = (rest - mid.astype(jnp.float32)).astype(jnp.bfloat16)
        return carry

    lax.fori_loop(0, modes, split, 0)
    tile, group = 2 * LANES, 8

    def gram(step, carry):
        cols = pl.ds(pl.multiple_of(step // (modes // group) * tile, tile), tile)
        first = step % (modes // group)
        rows = pl.ds(pl.multiple_of(first * group * modes, group * modes), group * modes)
        w = w_ref[:, cols]
        total = jnp.dot(lo_ref[rows, :], w, preferred_element_type=jnp.float32)
        total += jnp.dot(mid_ref[rows, :], w, preferred_element_type=jnp.float32)
        total += jnp.dot(hi_ref[rows, :], w, preferred_element_type=jnp.float32)
        l_ref[pl.ds(first * group, group), :, cols] = total.reshape(group, modes, tile)
        return carry

    lax.fori_loop(0, 2 * columns // tile * (modes // group), gram, 0)
    width = 4 * LANES

    def cholesky(step, carry):
        cols = pl.ds(pl.multiple_of(step * width, width), width)
        for k in range(modes):
            low = k // 8 * 8
            row = lax.broadcasted_iota(jnp.int32, (modes - low, width), 0) + low
            acc = l_ref[k, low:, cols] + jnp.where(row == k, damping, 0.0)
            for m in range(k):
                acc = acc - l_ref[m, low:, cols] * l_ref[m, k : k + 1, cols]
            inv = 1.0 / jnp.sqrt(acc[k - low : k - low + 1])
            inv_ref[k : k + 1, cols] = inv
            l_ref[k, low:, cols] = acc * inv
        return carry

    lax.fori_loop(0, 2 * columns // width, cholesky, 0)


def fit_kernel(chips, groups, vis_hbm, mask_hbm, share_ref, spread_ref, valid_ref, wide_ref, out_ref, loc_ref,
               vis_ref, own_ref, mask_ref, table, mt_all, w_ref, hi_ref, mid_ref, lo_ref, l_ref, inv_ref,
               give, keep, take, sums, come, sems, mask_sems, table_sems, local_sems):
    me, grp = lax.axis_index("chan"), lax.axis_index("grp")
    chip, core = me // 2, me % 2
    turn = 1 - 2 * (2 * chip // chips)
    modes, width = inv_ref.shape
    rows = vis_ref.shape[0]
    columns = mask_ref.shape[2]
    share = share_ref.shape[1]
    mate = chip * 2 + 1 - core

    def other(d):
        return lax.rem(chip + turn * d + chips, chips)

    load_own = pltpu.make_async_copy(mask_hbm, own_ref, local_sems.at[0])
    load_own.start()
    barrier = pltpu.get_barrier_semaphore()
    for d in range(1, 2 * chips):
        pl.semaphore_signal(barrier, inc=1, device_id={"chan": lax.rem(me + d, 2 * chips)}, device_id_type=MESH)
    for d in range(1, groups):
        pl.semaphore_signal(barrier, inc=1, device_id={"grp": lax.rem(grp + d, groups)}, device_id_type=MESH)
    pl.semaphore_wait(barrier, 2 * chips + groups - 2)

    def flags(peer, slot, at):
        return pltpu.make_async_remote_copy(
            src_ref=mask_hbm.at[pl.ds(pl.multiple_of(peer * rows, rows), rows)], dst_ref=mask_ref.at[slot],
            send_sem=mask_sems.at[0, peer], recv_sem=mask_sems.at[1, at],
            device_id={"chan": peer}, device_id_type=MESH)

    def modes_copy(peer, slot):
        return pltpu.make_async_remote_copy(
            src_ref=share_ref, dst_ref=table.at[slot], send_sem=table_sems.at[0, peer],
            recv_sem=table_sems.at[1, slot], device_id={"grp": peer}, device_id_type=MESH)

    for d in range(1, groups):
        modes_copy(lax.rem(grp + d, groups), grp).start()
    flags(mate, me, me).start()
    for d in range(1, chips):
        flags(other(d) * 2 + core, me, me).start()
        flags(other(d) * 2 + 1 - core, me, me).start()
    load_vis = pltpu.make_async_copy(vis_hbm, vis_ref, local_sems.at[1])
    load_vis.start()
    load_mine = pltpu.make_async_copy(
        mask_hbm.at[pl.ds(pl.multiple_of(me * rows, rows), rows)], mask_ref.at[me], local_sems.at[2])
    load_mine.start()

    table[grp] = share_ref[...]
    for d in range(1, groups):
        peer = lax.rem(grp + d, groups)
        modes_copy(peer, peer).wait_recv()
    for q in range(groups):
        mt_all[:, q * share : (q + 1) * share] = table[q]
    pick = lax.broadcasted_iota(jnp.int32, (groups * share, rows), 0)
    pick = pick == lax.broadcasted_iota(jnp.int32, (groups * share, rows), 1) + me * rows
    loc_ref[...] = jnp.dot(mt_all[...], pick.astype(jnp.float32),
                           precision=lax.Precision.HIGHEST, preferred_element_type=jnp.float32)
    load_own.wait()
    factor_kernel(mt_all, own_ref, valid_ref, spread_ref, l_ref, inv_ref, w_ref, hi_ref, mid_ref, lo_ref)
    load_vis.wait()
    load_mine.wait()

    def copy(stage, src, dst, slot, peer, at):
        return pltpu.make_async_remote_copy(
            src_ref=src, dst_ref=dst, send_sem=sems.at[2 * stage, slot], recv_sem=sems.at[2 * stage + 1, at],
            device_id={"chan": peer}, device_id_type=MESH)

    def project(owner, dst, slot):
        for j in range(columns // LANES):
            w = 1.0 - mask_ref[owner, :, j * LANES : (j + 1) * LANES].astype(jnp.float32)
            w = jnp.dot(w.astype(jnp.bfloat16), spread_ref[...], preferred_element_type=jnp.float32)
            at = pl.multiple_of(owner * width + 2 * j * LANES, 2 * LANES)
            v = vis_ref[:, pl.ds(at, 2 * LANES)] * w
            dst[slot, :, 2 * j * LANES : 2 * (j + 1) * LANES] = jnp.dot(
                loc_ref[...], v, precision=lax.Precision.HIGHEST, preferred_element_type=jnp.float32)

    flags(mate, mate, mate).wait_recv()
    project(mate, give, chip)
    pair = copy(0, give.at[chip], take.at[chip], chip, mate, chip)
    pair.start()
    project(me, keep, chip)
    pair.wait()

    def collect(d, carry):
        slot = other(d)
        first, second = slot * 2 + 1 - core, slot * 2 + core
        flags(first, first, first).wait_recv()
        project(first, give, slot)
        pair = copy(0, give.at[slot], take.at[slot], slot, mate, slot)
        pair.start()
        flags(second, second, second).wait_recv()
        project(second, keep, slot)
        pair.wait()
        sums[slot] = keep[slot] + take[slot]
        copy(1, sums.at[slot], come.at[chip], slot, slot * 2 + core, chip).start()
        return carry

    lax.fori_loop(1, chips, collect, 0)
    total = keep[chip] + take[chip]
    for d in range(1, chips):
        slot = other(d)
        copy(1, sums.at[slot], come.at[slot], slot, slot * 2 + core, slot).wait()
        total = total + come[slot]
    take[chip] = total * wide_ref[...]

    part = 2 * LANES

    def solve(step, carry):
        cols = pl.ds(pl.multiple_of(step * part, part), part)
        row = lax.broadcasted_iota(jnp.int32, (modes, part), 0)
        left = take[chip, :, cols]
        groups = [left[g * 8 : (g + 1) * 8] for g in range(modes // 8)]
        ys = []
        for k in range(modes):
            low = k // 8
            y = groups[low][k % 8 : k % 8 + 1] * inv_ref[k : k + 1, cols]
            ys.append(y)
            for g in range(low, modes // 8):
                groups[g] = groups[g] - l_ref[k, g * 8 : (g + 1) * 8, cols] * y
        row = lax.broadcasted_iota(jnp.int32, (8, part), 0)
        xs = [jnp.zeros((8, part), jnp.float32) for _ in range(modes // 8)]
        for k in reversed(range(modes)):
            low = k // 8
            acc = l_ref[k, low * 8 : (low + 1) * 8, cols] * xs[low]
            for g in range(low + 1, modes // 8):
                acc = acc + l_ref[k, g * 8 : (g + 1) * 8, cols] * xs[g]
            x = (ys[k] - jnp.sum(acc, axis=0, keepdims=True)) * inv_ref[k : k + 1, cols]
            xs[low] = jnp.where(row == k % 8, x, xs[low])
        for g in range(modes // 8):
            out_ref[me, g * 8 : (g + 1) * 8, cols] = xs[g]
        return carry

    lax.fori_loop(0, width // part, solve, 0)

    def spread(slot):
        block = out_ref.at[slot * 2 + core]
        return copy(3, block, block, slot, mate, slot)

    for d in range(1, chips):
        slot = lax.rem(chip + d, chips)
        copy(2, out_ref.at[me], out_ref.at[me], slot, slot * 2 + core, chip).start()
    spread(chip).start()
    for d in range(1, chips):
        slot = lax.rem(chip + d, chips)
        block = out_ref.at[slot * 2 + core]
        copy(2, block, block, slot, slot * 2 + core, slot).wait_recv()
        spread(slot).start()
    for d in range(1, chips):
        slot = lax.rem(chip + d, chips)
        copy(2, out_ref.at[me], out_ref.at[me], slot, slot * 2 + core, chip).wait_send()
    for slot in range(chips):
        block = out_ref.at[slot * 2 + 1 - core]
        spread(slot).wait_send()
        copy(3, block, block, slot, mate, slot).wait_recv()
    flags(mate, me, me).wait_send()
    for d in range(1, chips):
        flags(other(d) * 2 + core, me, me).wait_send()
        flags(other(d) * 2 + 1 - core, me, me).wait_send()
    for d in range(1, groups):
        modes_copy(lax.rem(grp + d, groups), grp).wait_send()


def pieces(x):
    hi = x.astype(jnp.bfloat16)
    rest = x - hi.astype(jnp.float32)
    mid = rest.astype(jnp.bfloat16)
    return hi, mid, (rest - mid.astype(jnp.float32)).astype(jnp.bfloat16)


def residual_kernel(vis_ref, modes_ref, coef_ref, out_ref):
    width = coef_ref.shape[2]
    hi, mid, lo = pieces(modes_ref[...])
    left = jnp.concatenate([hi, hi, mid, mid, hi, lo], axis=0)
    for j in range(coef_ref.shape[0]):
        cols = slice(j * width, (j + 1) * width)
        hi, mid, lo = pieces(coef_ref[j])
        right = jnp.concatenate([hi, mid, hi, mid, lo, hi], axis=0)
        out_ref[:, cols] = vis_ref[:, cols] - lax.dot_general(
            left, right, (((0,), (0,)), ((), ())), preferred_element_type=jnp.float32)


def per_device(chan, groups, visibility, interference_mask, valid_time_count, fit_modes):
    rows, all_columns = visibility.shape
    freqs, columns = interference_mask.shape
    share, modes = fit_modes.shape
    base = valid_time_count.shape[0]
    times = columns // base
    width = 2 * columns
    chips = chan // 2
    within = (lax.broadcasted_iota(jnp.int32, (base, times), 1) < valid_time_count[:, None]).astype(jnp.float32)
    valid = within.reshape(1, columns)
    valid_wide = jnp.broadcast_to(within[:, None, :], (base, 2, times)).reshape(1, width)
    source = lax.broadcasted_iota(jnp.int32, (LANES, 2 * LANES), 0)
    column = lax.broadcasted_iota(jnp.int32, (LANES, 2 * LANES), 1)
    spread = (source == column // (2 * times) * times + column % times).astype(jnp.bfloat16)
    f32, bf16 = jnp.float32, jnp.bfloat16
    block = pltpu.VMEM((chips, modes, width), f32)
    anywhere = pl.BlockSpec(memory_space=pl.ANY)
    coefficients, local = pl.pallas_call(
        functools.partial(fit_kernel, chips, groups),
        out_shape=(jax.ShapeDtypeStruct((chan, modes, width), f32), jax.ShapeDtypeStruct((modes, rows), f32)),
        in_specs=[anywhere] * 2 + [VMEM] * 4,
        out_specs=(VMEM, VMEM),
        scratch_shapes=[
            pltpu.VMEM((rows, all_columns), f32),
            pltpu.VMEM((freqs, columns), jnp.int32),
            pltpu.VMEM((chan, rows, columns), jnp.int32),
            pltpu.VMEM((groups, modes, share), f32),
            pltpu.VMEM((modes, freqs), f32),
            pltpu.VMEM((freqs, width), bf16),
        ]
        + [pltpu.VMEM((modes * modes, freqs), bf16)] * 3
        + [pltpu.VMEM((modes, modes, width), f32), pltpu.VMEM((modes, width), f32)]
        + [block] * 5
        + [pltpu.SemaphoreType.DMA((8, chips)), pltpu.SemaphoreType.DMA((2, chan)),
           pltpu.SemaphoreType.DMA((2, groups)), pltpu.SemaphoreType.DMA((3,))],
        compiler_params=pltpu.CompilerParams(
            collective_id=0, has_side_effects=True, vmem_limit_bytes=61 << 20),
        cost_estimate=pl.CostEstimate(flops=10**10, bytes_accessed=12 << 20, transcendentals=0),
        name="fit",
    )(visibility, interference_mask, fit_modes.T, spread, valid, valid_wide)
    step = 2
    return pl.pallas_call(
        residual_kernel,
        grid=(chan // step,),
        out_shape=jax.ShapeDtypeStruct((rows, all_columns), f32),
        in_specs=[
            pl.BlockSpec((rows, step * width), lambda i: (0, i)),
            pl.BlockSpec((modes, rows), lambda i: (0, 0)),
            pl.BlockSpec((step, modes, width), lambda i: (i, 0, 0)),
        ],
        out_specs=pl.BlockSpec((rows, step * width), lambda i: (0, i)),
        name="residual",
    )(visibility, local, coefficients)


def solution(mesh):
    placed = (P("chan", "grp"), P(None, ("grp", "chan")), P(("grp", "chan")), P("grp", None))
    return jax.shard_map(
        functools.partial(per_device, mesh.shape["chan"], mesh.shape["grp"]), mesh=mesh, in_specs=placed,
        out_specs=P("chan", "grp"), check_vma=False)
```

profile of v0, /device:TPU:0, one launch (start us, length us, event | category | flops | bytes accessed | tf_op | source)
XLA Modules:
  0.0 85.0 jit_solution(14063311493966044461)
XLA Ops:
  0.0 0.7 fusion.1
  0.8 0.7 reshape.47.valid_ref
  1.4 0.7 reshape.46.wide_ref
  2.1 0.6 fusion.spread_ref
  2.7 76.6 %fit.1 = (f32[8,32,1024]{2,1,0:T(8,128)}, f32[32,128]{1,0:T(8,128)}) custom-call(f32[128,8192]{1,0:T(8,128)} %vis_ref.1, s32[1024,512]{1,0:T(8,128)} %mask_hbm.1, f32[32,256]{1,0:T(8,128)} %bitcast.1, bf16[128,256]{1,0:T(8,128)(2,1)} %fusion.spread_ref, f32[1,512]{1,0:T(1,128)} %reshape.47.valid_ref, f32[1,1024]{1,0:T(1,128)} %reshape.46.wide_ref), custom_call_target="tpu_custom_call" | custom-call | flops 10000000000 | bytes 12582912 | tf_op jit(solution)/shard_map/fit/pallas_call | solution.py:268
  79.4 5.6 %residual.1 = f32[128,8192]{1,0:T(8,128)} custom-call(f32[128,8192]{1,0:T(8,128)} %vis_ref.1, f32[32,128]{1,0:T(8,128)} %get-tuple-element.7.modes_ref, f32[8,32,1024]{2,1,0:T(8,128)} %get-tuple-element.8.coef_ref), custom_call_target="tpu_custom_call" | custom-call | tf_op jit(solution)/shard_map/residual/pallas_call | solution.py:292
  (4 shorter events, 0.0 us)
where the time goes:
time: 86.2 us; the launch traced here: 85 us
  Pallas kernels  82.2 us (95%)
  other arithmetic  1.39 us (2%)
  local copies, waits for them, and re-layouts  1.35 us (2%)
    pallas_call x1, Pallas kernels, per_device(): pl.pallas_call(functools.partial(fit_kernel, chips, groups), out_shape=(j...  76.6 us
    pallas_call x1, Pallas kernels, per_device(): pl.pallas_call(residual_kernel, grid=(chan // step,), out_shape=jax.Shape...  5.56 us

commit v1 on v0

v1 whole, which is shorter than its diff:
```python
import functools
import math

import jax
import jax.numpy as jnp
from jax import lax
from jax.experimental import pallas as pl
from jax.experimental.pallas import tpu as pltpu
from jax.sharding import PartitionSpec as P

damping = 0.1
LANES = 128
VMEM = pl.BlockSpec(memory_space=pltpu.VMEM)
MESH = pl.DeviceIdType.MESH
f32, bf16 = jnp.float32, jnp.bfloat16


def pieces(x):
    hi = x.astype(bf16)
    rest = x - hi.astype(f32)
    mid = rest.astype(bf16)
    return hi, mid, (rest - mid.astype(f32)).astype(bf16)


def factor_kernel(mt_ref, mask_ref, valid, spread, l_ref, inv_ref, w_ref, hi_ref, mid_ref, lo_ref):
    modes, freqs = mt_ref.shape
    columns = mask_ref.shape[1]
    for j in range(columns // LANES):
        part = slice(j * LANES, (j + 1) * LANES)
        w = (1.0 - mask_ref[:, part].astype(f32)) * valid[:, part]
        w_ref[:, 2 * j * LANES : 2 * (j + 1) * LANES] = jnp.dot(
            w.astype(bf16), spread, preferred_element_type=f32
        ).astype(bf16)

    def split(i, carry):
        rows = pl.ds(pl.multiple_of(i * modes, modes), modes)
        hi_ref[rows, :], mid_ref[rows, :], lo_ref[rows, :] = pieces(mt_ref[...] * mt_ref[pl.ds(i, 1), :])
        return carry

    lax.fori_loop(0, modes, split, 0)
    tile, group = 2 * LANES, 8

    def gram(step, carry):
        cols = pl.ds(pl.multiple_of(step // (modes // group) * tile, tile), tile)
        first = step % (modes // group)
        rows = pl.ds(pl.multiple_of(first * group * modes, group * modes), group * modes)
        w = w_ref[:, cols]
        total = jnp.dot(lo_ref[rows, :], w, preferred_element_type=f32)
        total += jnp.dot(mid_ref[rows, :], w, preferred_element_type=f32)
        total += jnp.dot(hi_ref[rows, :], w, preferred_element_type=f32)
        l_ref[pl.ds(first * group, group), :, cols] = total.reshape(group, modes, tile)
        return carry

    lax.fori_loop(0, 2 * columns // tile * (modes // group), gram, 0)
    width = 4 * LANES

    def cholesky(step, carry):
        cols = pl.ds(pl.multiple_of(step * width, width), width)
        for k in range(modes):
            low = k // 8 * 8
            row = lax.broadcasted_iota(jnp.int32, (modes - low, width), 0) + low
            acc = l_ref[k, low:, cols] + jnp.where(row == k, damping, 0.0)
            for m in range(k):
                acc = acc - l_ref[m, low:, cols] * l_ref[m, k : k + 1, cols]
            inv = 1.0 / jnp.sqrt(acc[k - low : k - low + 1])
            inv_ref[k : k + 1, cols] = inv
            l_ref[k, low:, cols] = acc * inv
        return carry

    lax.fori_loop(0, 2 * columns // width, cholesky, 0)


def fit_kernel(chips, groups, vis_hbm, mask_hbm, count_hbm, share_hbm, out_ref,
               vis_ref, own_ref, mask_ref, counts, mt_all, loc_ref, left_ref, w_ref, hi_ref, mid_ref, lo_ref,
               l_ref, inv_ref, give, keep, take, fwd, come, coef,
               pair_sems, fwd_sems, come_sems, near_sems, relay_sems, mate_sems, mask_sems, table_sems, local_sems):
    me, grp = lax.axis_index("chan"), lax.axis_index("grp")
    chip, core = me // 2, me % 2
    pairs = chips // 2
    pair, side = chip // 2, chip % 2
    partner = chip + 1 - 2 * side
    mate = chip * 2 + 1 - core
    turn = 1 - 2 * (2 * chip // chips)
    modes, width = inv_ref.shape
    rows = vis_ref.shape[0]
    chunks, tile = keep.shape[0], keep.shape[3]
    columns = own_ref.shape[1]
    share = share_hbm.shape[1]
    bases = counts.shape[0]
    times = columns // bases

    def other(d):
        return lax.rem(chip + turn * d + chips, chips)

    def toward(slot):
        return jnp.logical_or(jnp.logical_and(slot // 2 > pair, side == 1), jnp.logical_and(slot // 2 < pair, side == 0))

    def nearest(p):
        return jnp.where(p == pair, partner, jnp.where(p > pair, 2 * p, 2 * p + 1))

    load_share = pltpu.make_async_copy(share_hbm, mt_all.at[:, pl.ds(pl.multiple_of(grp * share, share), share)], local_sems.at[3])
    load_share.start()
    load_counts = pltpu.make_async_copy(count_hbm, counts, local_sems.at[4])
    load_counts.start()
    load_own = pltpu.make_async_copy(mask_hbm, own_ref, local_sems.at[0])
    load_own.start()
    barrier = pltpu.get_barrier_semaphore()
    for d in range(1, 2 * chips):
        pl.semaphore_signal(barrier, inc=1, device_id={"chan": lax.rem(me + d, 2 * chips)}, device_id_type=MESH)
    for d in range(1, groups):
        pl.semaphore_signal(barrier, inc=1, device_id={"grp": lax.rem(grp + d, groups)}, device_id_type=MESH)
    pl.semaphore_wait(barrier, 2 * chips + groups - 2)

    def flags(k, peer, slot):
        return pltpu.make_async_remote_copy(
            src_ref=mask_hbm.at[pl.ds(pl.multiple_of(peer * rows, rows), rows), pl.ds(pl.multiple_of(k * LANES, LANES), LANES)],
            dst_ref=mask_ref.at[slot, k], send_sem=mask_sems.at[0, k, peer], recv_sem=mask_sems.at[1, k, slot],
            device_id={"chan": peer}, device_id_type=MESH)

    def modes_copy(peer, slot):
        return pltpu.make_async_remote_copy(
            src_ref=share_hbm, dst_ref=mt_all.at[:, pl.ds(pl.multiple_of(slot * share, share), share)],
            send_sem=table_sems.at[0, peer], recv_sem=table_sems.at[1, slot], device_id={"grp": peer}, device_id_type=MESH)

    def send_flags(k):
        flags(k, mate, me).start()

        def send(d, carry):
            flags(k, other(d) * 2 + core, me).start()
            flags(k, other(d) * 2 + 1 - core, me).start()
            return carry

        lax.fori_loop(1, chips, send, 0)

    ahead = min(2, chunks)
    for d in range(1, groups):
        modes_copy(lax.rem(grp + d, groups), grp).start()
    for k in range(ahead):
        send_flags(k)
    inner = jnp.logical_or(jnp.logical_and(side == 1, pair == 0), jnp.logical_and(side == 0, pair == pairs - 1))

    @pl.when(inner)
    def _():
        for k in range(ahead, chunks):
            send_flags(k)

    load_vis = pltpu.make_async_copy(vis_hbm, vis_ref, local_sems.at[1])
    load_vis.start()

    def load_mine(k):
        return pltpu.make_async_copy(
            mask_hbm.at[pl.ds(pl.multiple_of(me * rows, rows), rows), k * LANES : (k + 1) * LANES],
            mask_ref.at[me, k], local_sems.at[5 + k])

    for k in range(chunks):
        load_mine(k).start()

    source = lax.broadcasted_iota(jnp.int32, (LANES, 2 * LANES), 0)
    column = lax.broadcasted_iota(jnp.int32, (LANES, 2 * LANES), 1)
    spread = jnp.where(source == column // (2 * times) * times + column % times, 1.0, 0.0).astype(bf16)
    load_counts.wait()
    lane = lax.broadcasted_iota(jnp.int32, (1, columns), 1)
    held = jnp.zeros((1, columns), jnp.int32)
    for b in range(bases):
        held = jnp.where(lane // times == b, counts[b], held)
    valid = jnp.where(lane % times < held, 1.0, 0.0)
    lane = lax.broadcasted_iota(jnp.int32, (1, width), 1)
    held = jnp.zeros((1, width), jnp.int32)
    for b in range(bases):
        held = jnp.where(lane // (2 * times) == b, counts[b], held)
    valid_wide = jnp.where(lane % times < held, 1.0, 0.0)

    load_share.wait()
    for d in range(1, groups):
        peer = lax.rem(grp + d, groups)
        modes_copy(peer, peer).wait_recv()
    pick = lax.broadcasted_iota(jnp.int32, (groups * share, rows), 0)
    pick = pick == lax.broadcasted_iota(jnp.int32, (groups * share, rows), 1) + me * rows
    loc = jnp.dot(mt_all[...], pick.astype(f32), precision=lax.Precision.HIGHEST, preferred_element_type=f32)
    loc_ref[...] = loc
    hi, mid, lo = pieces(loc)
    left_ref[...] = jnp.concatenate([hi, hi, mid, mid, hi, lo], axis=0)
    load_own.wait()
    factor_kernel(mt_all, own_ref, valid, spread, l_ref, inv_ref, w_ref, hi_ref, mid_ref, lo_ref)
    load_vis.wait()
    for k in range(chunks):
        load_mine(k).wait()

    def remote(src, dst, send, recv, peer):
        return pltpu.make_async_remote_copy(
            src_ref=src, dst_ref=dst, send_sem=send, recv_sem=recv, device_id={"chan": peer}, device_id_type=MESH)

    def swap(k, slot):
        return remote(give.at[k, slot], take.at[k, slot], pair_sems.at[0, k, slot], pair_sems.at[1, k, slot], mate)

    def pass_on(k, slot):
        return remote(keep.at[k, slot], fwd.at[k, slot], fwd_sems.at[0, k, slot], fwd_sems.at[1, k, slot], partner * 2 + core)

    def deliver(k, slot, at):
        return remote(keep.at[k, slot], come.at[k, at], come_sems.at[0, k, slot], come_sems.at[1, k, at], slot * 2 + core)

    def vis_at(owner, k):
        return pl.ds(pl.multiple_of(owner * width + k * tile, tile), tile)

    def project(owner, k):
        w = 1.0 - mask_ref[owner, k].astype(f32)
        w = jnp.dot(w.astype(bf16), spread, preferred_element_type=f32)
        return jnp.dot(loc_ref[...], vis_ref[:, vis_at(owner, k)] * w,
                       precision=lax.Precision.HIGHEST, preferred_element_type=f32)

    def near_pair(slot):
        return jnp.logical_and(slot // 2 == pair, slot != chip)

    def passed(slot):
        return jnp.logical_and(slot // 2 != pair, jnp.logical_not(toward(slot)))

    def chunk(k, carry):
        def partial(d, c):
            slot = other(d)
            first, second = slot * 2 + 1 - core, slot * 2 + core
            flags(k, first, first).wait_recv()
            give[k, slot] = project(first, k)
            swap(k, slot).start()

            @pl.when(d > 0)
            def _():
                flags(k, second, second).wait_recv()

            keep[k, slot] = project(second, k)
            return c

        lax.fori_loop(0, chips, partial, 0)

        def merge(d, c):
            slot = other(d)
            swap(k, slot).wait()
            keep[k, slot] = keep[k, slot] + take[k, slot]

            @pl.when(near_pair(slot))
            def _():
                deliver(k, slot, pair).start()

            @pl.when(passed(slot))
            def _():
                pass_on(k, slot).start()

            return c

        lax.fori_loop(0, chips, merge, 0)

        @pl.when(jnp.logical_and(jnp.logical_not(inner), k + ahead < chunks))
        def _():
            send_flags(k + ahead)

        @pl.when(k > 0)
        def _():
            join(k - 1)

        return carry

    def join(k):
        def step(d, c):
            slot = other(d)

            @pl.when(toward(slot))
            def _():
                pass_on(k, slot).wait_recv()
                keep[k, slot] = keep[k, slot] + fwd[k, slot]
                deliver(k, slot, pair).start()

            return c

        lax.fori_loop(1, chips, step, 0)

    lax.fori_loop(0, chunks, chunk, 0)
    join(chunks - 1)

    def near(k, p):
        block = coef.at[k, me]
        peer = nearest(p)
        return remote(block, block, near_sems.at[0, k, p], near_sems.at[1, k, chip], peer * 2 + core)

    def arrived(k, slot):
        block = coef.at[k, slot * 2 + core]
        return remote(block, block, near_sems.at[0, k, 0], near_sems.at[1, k, slot], slot * 2 + core)

    def relay(k, slot):
        block = coef.at[k, slot * 2 + core]
        return remote(block, block, relay_sems.at[k, slot], near_sems.at[1, k, slot], partner * 2 + core)

    def to_mate(k, slot):
        block = coef.at[k, slot * 2 + core]
        return remote(block, block, mate_sems.at[0, k, slot], mate_sems.at[1, k, slot], mate)

    def from_mate(k, slot):
        block = coef.at[k, slot * 2 + 1 - core]
        return remote(block, block, mate_sems.at[0, k, slot], mate_sems.at[1, k, slot], mate)

    def solve(k):
        total = keep[k, chip]
        for p in range(pairs):
            deliver(k, chip, p).wait_recv()
            total = total + come[k, p]
        cols = pl.ds(k * tile, tile)
        left = total * valid_wide[:, k * tile : (k + 1) * tile]
        parts = [left[g * 8 : (g + 1) * 8] for g in range(modes // 8)]
        ys = []
        for m in range(modes):
            low = m // 8
            y = parts[low][m % 8 : m % 8 + 1] * inv_ref[m : m + 1, cols]
            ys.append(y)
            for g in range(low, modes // 8):
                parts[g] = parts[g] - l_ref[m, g * 8 : (g + 1) * 8, cols] * y
        row = lax.broadcasted_iota(jnp.int32, (8, tile), 0)
        xs = [jnp.zeros((8, tile), f32) for _ in range(modes // 8)]
        for m in reversed(range(modes)):
            low = m // 8
            acc = l_ref[m, low * 8 : (low + 1) * 8, cols] * xs[low]
            for g in range(low + 1, modes // 8):
                acc = acc + l_ref[m, g * 8 : (g + 1) * 8, cols] * xs[g]
            x = (ys[m] - jnp.sum(acc, axis=0, keepdims=True)) * inv_ref[m : m + 1, cols]
            xs[low] = jnp.where(row == m % 8, x, xs[low])
        for g in range(modes // 8):
            coef[k, me, g * 8 : (g + 1) * 8, :] = xs[g]
        for p in range(pairs):
            near(k, p).start()
        to_mate(k, chip).start()

    def spread_coef(k):
        def step(d, c):
            slot = other(d)
            arrived(k, slot).wait_recv()

            @pl.when(toward(slot))
            def _():
                relay(k, slot).start()

            to_mate(k, slot).start()
            return c

        lax.fori_loop(1, chips, step, 0)

    def subtract(owner, k):
        hi, mid, lo = pieces(coef[k, owner])
        right = jnp.concatenate([hi, mid, hi, mid, lo, hi], axis=0)
        cols = vis_at(owner, k)
        out_ref[:, cols] = vis_ref[:, cols] - lax.dot_general(
            left_ref[...], right, (((0,), (0,)), ((), ())), preferred_element_type=f32)

    def residual(k):
        def step(d, c):
            slot = other(d)
            subtract(slot * 2 + core, k)
            from_mate(k, slot).wait_recv()
            subtract(slot * 2 + 1 - core, k)
            return c

        lax.fori_loop(0, chips, step, 0)

    for k in range(chunks):
        solve(k)
        if k > 0:
            spread_coef(k - 1)
            residual(k - 1)
    spread_coef(chunks - 1)
    residual(chunks - 1)

    def finish(k, carry):
        flags(k, mate, me).wait_send()
        for p in range(pairs):
            near(k, p).wait_send()

        def step(d, c):
            slot = other(d)
            to_mate(k, slot).wait_send()

            @pl.when(d > 0)
            def _():
                flags(k, slot * 2 + core, me).wait_send()
                flags(k, slot * 2 + 1 - core, me).wait_send()

            @pl.when(passed(slot))
            def _():
                pass_on(k, slot).wait_send()

            @pl.when(jnp.logical_or(near_pair(slot), toward(slot)))
            def _():
                deliver(k, slot, pair).wait_send()

            @pl.when(toward(slot))
            def _():
                relay(k, slot).wait_send()

            return c

        lax.fori_loop(0, chips, step, 0)
        return carry

    lax.fori_loop(0, chunks, finish, 0)
    for d in range(1, groups):
        modes_copy(lax.rem(grp + d, groups), grp).wait_send()


def per_device(chan, groups, visibility, interference_mask, valid_time_count, fit_modes):
    rows, all_columns = visibility.shape
    freqs, columns = interference_mask.shape
    share, modes = fit_modes.shape
    bases = valid_time_count.shape[0]
    width = 2 * columns
    chips = chan // 2
    chunks, tile = columns // LANES, 2 * LANES
    block = pltpu.VMEM((chunks, chips, modes, tile), f32)
    anywhere = pl.BlockSpec(memory_space=pltpu.HBM)
    dma = pltpu.SemaphoreType.DMA
    scratch = (
        [
            pltpu.VMEM((rows, all_columns), f32),
            pltpu.VMEM((freqs, columns), jnp.int32),
            pltpu.VMEM((chan, chunks, rows, LANES), jnp.int32),
            pltpu.SMEM((bases,), jnp.int32),
            pltpu.VMEM((modes, freqs), f32),
            pltpu.VMEM((modes, rows), f32),
            pltpu.VMEM((6 * modes, rows), bf16),
            pltpu.VMEM((freqs, width), bf16),
        ]
        + [pltpu.VMEM((modes * modes, freqs), bf16)] * 3
        + [pltpu.VMEM((modes, modes, width), f32), pltpu.VMEM((modes, width), f32)]
        + [block] * 4
        + [pltpu.VMEM((chunks, chips // 2, modes, tile), f32), pltpu.VMEM((chunks, chan, modes, tile), f32)]
        + [dma((2, chunks, chips))] * 3
        + [dma((2, chunks, chips)), dma((chunks, chips)), dma((2, chunks, chips)), dma((2, chunks, chan)),
           dma((2, groups)), dma((5 + chunks,))]
    )
    held = sum(math.prod(s.shape) * jnp.dtype(s.dtype).itemsize for s in scratch[:-9])
    return pl.pallas_call(
        functools.partial(fit_kernel, chips, groups),
        out_shape=jax.ShapeDtypeStruct((rows, all_columns), f32),
        in_specs=[anywhere] * 4,
        out_specs=VMEM,
        scratch_shapes=scratch,
        compiler_params=pltpu.CompilerParams(
            collective_id=0, has_side_effects=True, vmem_limit_bytes=held + (5 << 20)),
        cost_estimate=pl.CostEstimate(flops=10**10, bytes_accessed=12 << 20, transcendentals=0),
        name="fit",
    )(*[pltpu.with_memory_space_constraint(a, pltpu.HBM)
        for a in (visibility, interference_mask, valid_time_count, fit_modes.T)])


def solution(mesh):
    placed = (P("chan", "grp"), P(None, ("grp", "chan")), P(("grp", "chan")), P("grp", None))
    return jax.shard_map(
        functools.partial(per_device, mesh.shape["chan"], mesh.shape["grp"]), mesh=mesh, in_specs=placed,
        out_specs=P("chan", "grp"), check_vma=False)
```

time: 86.2 us -> 84.8 us (0.984); the launches traced: 85 us -> 84.6 us
  other arithmetic: 1.39 us -> 0 us
    unnamed x0 -> x1, local copies, waits for them, and re-layouts: none -> 2.02 us
    convert_element_type x2 -> x0, other arithmetic: 1.38 us -> none  [the longest x1 0.73 us: per_device(): (lax.broadcasted_iota(jnp.int32, (base, times), 1) < valid_time_count[:,...]
    pallas_call x2 -> x1, Pallas kernels: 82.2 us -> 82.6 us  [per_device(): pl.pallas_call(functools.partial(fit_kernel, chips, groups), out_shape=ja...]
where the time goes in v1:
time: 84.8 us; the launch traced here: 84.6 us
  Pallas kernels  82.6 us (97%)
  local copies, waits for them, and re-layouts  2.02 us (2%)
    pallas_call x1, Pallas kernels, per_device(): pl.pallas_call(functools.partial(fit_kernel, chips, groups), out_shape=ja...  82.6 us
    unnamed x1, local copies, waits for them, and re-layouts  2.02 us

profile of v1, /device:TPU:0, one launch (start us, length us, event | category | flops | bytes accessed | tf_op | source)
XLA Modules:
  0.0 84.6 jit_solution(17643697274450759916)
XLA Ops:
  0.0 82.6 %fit.1 = f32[128,8192]{1,0:T(8,128)S(1)} custom-call(f32[128,8192]{1,0:T(8,128)} %vis_hbm.1, s32[1024,512]{1,0:T(8,128)} %mask_hbm.1, s32[16]{0:T(128)} %count_hbm.1, f32[32,256]{1,0:T(8,128)} %bitcast.1), custom_call_target="tpu_custom_call" | custom-call | flops 10000000000 | bytes 12582912 | tf_op jit(solution)/shard_map/fit/pallas_call | solution.py:435
  82.6 2.0 %copy.6 = f32[128,8192]{1,0:T(8,128)} copy(f32[128,8192]{1,0:T(8,128)S(1)} %fit.1) | data formatting | bytes 8388608
